TPU v7x, 32 devices: a whole 2x2x4 slice. The times are simulated.
32 devices in a mesh: client: 32 (over z, y, x, core).
Axes of the slice: x: 2, y: 2, z: 4, core: 2. Of those that a mesh axis runs over, the one named last changes fastest.
Arguments:
- patches: bfloat16 [4096, 192], P('client'), may hold values from -6 to 6
- labels: int32 [256], replicated, may hold values from 0 to 9
- assign: int32 [32, 1], replicated, may hold values from 0 to 15; in each aligned block of 32 rows (0 to 31, 32 to 63, ...) at most 4 rows name the same one
- patch_embed: bfloat16 [192, 384], replicated, may hold values from -0.4375 to 0.4375
- positions: bfloat16 [16, 384], replicated, may hold values from -3 to 3
- client_in: bfloat16 [384, 3072], replicated, may hold values from -3 to 3
- client_down: bfloat16 [1536, 384], replicated, may hold values from -0.15625 to 0.15625
- server_in: bfloat16 [2, 6144, 3072], P(None, 'client'), may hold values from -3 to 3
- server_down: bfloat16 [2, 24576, 384], P(None, 'client'), may hold values from -0.15625 to 0.15625
- classifier: bfloat16 [16, 384, 10], replicated, may hold values from -15 to 15
Outputs:
- losses: float32 [32, 16], P('client')
- grad_patch_embed: float32 [192, 384], P(None, 'client')
- grad_positions: float32 [16, 384], P(None, 'client')
- grad_client_in: float32 [384, 3072], P(None, 'client')
- grad_client_down: float32 [1536, 384], P(None, 'client')
- grad_server_in: float32 [2, 6144, 3072], P(None, 'client')
- grad_server_down: float32 [2, 24576, 384], P(None, 'client')
- grad_classifier: float32 [6144, 10], P('client')
Inputs may be any that keep to these rules, and one draw needn't show every extreme that they name: `assign`: no server shard is named by more than 4 clients, a bound that some block reaches.
All inputs are finite; a program needn't handle non-finite values.
Results may differ from a plain program's by a relative error of at most 0.025.
Values may be sent and summed in bfloat16 or wider, within the bound.
A program may use at most 128 MiB of HBM per device.

v0:
```python
import math

import jax
import jax.numpy as jnp
from jax import lax
from jax.sharding import PartitionSpec as P

D = 384
HEADS = 6
FF = 1536
TOK = 16
CLASSES = 10
IMG = 8
SHARDS = 16
SLOTS = 2
SERVER_LAYERS = 2


EPSILON = 1e-06


def partner_2(block, axis, apart):
    count = lax.axis_size(axis)
    route = []
    for low in range(count):
        high = low | 1 << apart
        if high != low and high < count:
            route += [(low, high), (high, low)]
    return lax.ppermute(block, axis, route)


def layer_norm(inputs):
    centre = inputs - jnp.mean(inputs, axis=-1, keepdims=True)
    spread = jnp.mean(centre * centre, axis=-1, keepdims=True)
    return centre * lax.rsqrt(spread + EPSILON)


def encoder_block(stream, weight_in, weight_down):
    images, tokens, model_width = stream.shape
    head_dim = model_width // HEADS
    normed = layer_norm(stream).astype(jnp.bfloat16).reshape(images * tokens, model_width)
    projected = jnp.dot(normed, weight_in[:, : 3 * model_width], preferred_element_type=jnp.float32)
    projected = projected.reshape(images, tokens, 3, HEADS, head_dim)
    queries = projected[:, :, 0]
    key_rows = projected[:, :, 1]
    values = projected[:, :, 2]
    scores = jnp.einsum(
        "bqhe,bkhe->bhqk", queries, key_rows, precision=lax.Precision.HIGHEST
    ) / math.sqrt(head_dim)
    weights_attn = jax.nn.softmax(scores, axis=-1)
    attended = jnp.einsum("bhqk,bkhe->bqhe", weights_attn, values, precision=lax.Precision.HIGHEST)
    attended = attended.reshape(images * tokens, model_width).astype(jnp.bfloat16)
    stream = stream + jnp.dot(
        attended,
        weight_in[:, 3 * model_width : 4 * model_width],
        preferred_element_type=jnp.float32,
    ).reshape(images, tokens, model_width)
    normed = layer_norm(stream).astype(jnp.bfloat16).reshape(images * tokens, model_width)
    hidden = jax.nn.gelu(
        jnp.dot(normed, weight_in[:, 4 * model_width :], preferred_element_type=jnp.float32)
    ).astype(jnp.bfloat16)
    return stream + jnp.dot(hidden, weight_down, preferred_element_type=jnp.float32).reshape(
        images, tokens, model_width
    )


def client_forward(patch_rows, patch_embed, positions, client_in, client_down):
    stream = jnp.dot(patch_rows, patch_embed, preferred_element_type=jnp.float32).reshape(
        -1, TOK, D
    )
    stream = stream + positions.astype(jnp.float32)
    stream = encoder_block(stream, client_in, client_down)
    return stream.reshape(-1, D).astype(jnp.bfloat16)


def server_loss(cut_rows, slot_hot, weights_in, weights_down, class_shard):
    stream = cut_rows.astype(jnp.float32).reshape(-1, TOK, D)
    for layer in range(len(weights_in)):
        stream = encoder_block(stream, weights_in[layer], weights_down[layer])
    pooled = layer_norm(jnp.mean(stream, axis=1)).astype(jnp.bfloat16)
    logits = jnp.dot(pooled, class_shard, preferred_element_type=jnp.float32)
    per_loss = (jax.nn.logsumexp(logits, axis=-1) - jnp.sum(slot_hot * logits, axis=-1)) * jnp.sum(
        slot_hot, axis=-1
    )
    return (jnp.sum(per_loss), per_loss)


def arrival_rank(routes):
    places = jnp.arange(routes.shape[0], dtype=jnp.int32)
    earlier = (routes[:, None] == routes[None, :]) & (places[:, None] < places[None, :])
    return jnp.sum(earlier.astype(jnp.int32), axis=0)


def select_matrix(routes, arrival, shard, capacity):
    slots_here = jnp.arange(capacity, dtype=jnp.int32)[:, None]
    return ((routes[None, :] == shard) & (arrival[None, :] == slots_here)).astype(jnp.bfloat16)


def slot_labels(labels, selector, rank_in_group, per_image, members):
    label_table = labels.reshape(members, IMG)
    label_part = lax.dynamic_slice_in_dim(label_table, rank_in_group * per_image, per_image, 1)
    onehot = (label_part[:, :, None] == jnp.arange(CLASSES, dtype=jnp.int32)[None, None, :]).astype(
        jnp.float32
    )
    onehot = onehot.reshape(members, per_image * CLASSES)
    chosen = jnp.dot(selector.astype(jnp.float32), onehot, precision=lax.Precision.HIGHEST)
    return chosen.reshape(-1, CLASSES)


def gather_group(flat_rows, group_bits, rank_in_group):
    stacked = flat_rows[None]
    for step_bit in range(group_bits):
        partner = partner_2(stacked, "client", step_bit)
        upper_half = rank_in_group >> step_bit & 1
        stacked = jnp.where(
            upper_half == 0,
            jnp.concatenate([stacked, partner], 0),
            jnp.concatenate([partner, stacked], 0),
        )
    return stacked


def reduce_group(blocks, group_bits, rank_in_group, order_bits):
    shaped = blocks.reshape((2,) * group_bits + (blocks.shape[1],))
    for step_bit in order_bits:
        axis_pos = group_bits - 1 - step_bit
        upper_half = rank_in_group >> step_bit & 1
        keeping = lax.dynamic_slice_in_dim(shaped, upper_half, 1, axis_pos)
        sending = lax.dynamic_slice_in_dim(shaped, 1 - upper_half, 1, axis_pos)
        shaped = keeping + partner_2(sending.astype(jnp.bfloat16), "client", step_bit).astype(
            sending.dtype
        )
    return shaped.reshape(-1)


def per_device(
    patches,
    labels,
    assign,
    patch_embed,
    positions,
    client_in,
    client_down,
    server_in,
    server_down,
    classifier,
):
    members = lax.axis_size("client")
    group_size = members // SHARDS
    group_bits = group_size.bit_length() - 1
    device_index = lax.axis_index("client")
    rank_in_group = device_index % group_size
    shard_here = device_index // group_size
    per_image = IMG // group_size
    piece_rows = IMG * TOK // group_size
    capacity = SLOTS * group_size
    width_all = 4 * D + FF
    rows_in = D // group_size
    rows_down = FF // group_size
    routes = assign[:, 0]
    places = jnp.arange(members, dtype=jnp.int32)
    own_shard = jnp.sum(jnp.where(places == device_index, routes, 0))

    def client_of(embed_weights, position_weights, in_weights, down_weights):
        return client_forward(patches, embed_weights, position_weights, in_weights, down_weights)

    cut_acts, client_back = jax.vjp(client_of, patch_embed, positions, client_in, client_down)
    pieces = cut_acts.reshape(group_size, piece_rows, D)
    tiled = jnp.broadcast_to(pieces[None], (SHARDS, group_size, piece_rows, D)).reshape(
        members, piece_rows, D
    )
    target = places // group_size == own_shard
    outgoing = jnp.where(target[:, None, None], tiled, jnp.zeros_like(tiled))
    arrived = lax.all_to_all(outgoing, "client", split_axis=0, concat_axis=0, tiled=True)
    arrival = arrival_rank(routes)
    selector = select_matrix(routes, arrival, shard_here, capacity)
    compact = jnp.dot(
        selector, arrived.reshape(members, piece_rows * D), preferred_element_type=jnp.float32
    )
    compact = compact.astype(jnp.bfloat16).reshape(capacity * piece_rows, D)
    slot_hot = slot_labels(labels, selector, rank_in_group, per_image, members)
    weights_in = []
    weights_down = []
    size_in = SERVER_LAYERS * rows_in * width_all
    flat_rows = jnp.concatenate([server_in.reshape(-1), server_down.reshape(-1)])
    stacked = gather_group(flat_rows, group_bits, rank_in_group)
    whole_in = stacked[:, :size_in].reshape(group_size, SERVER_LAYERS, rows_in, width_all)
    whole_in = whole_in.transpose(1, 0, 2, 3).reshape(SERVER_LAYERS, D, width_all)
    whole_down = stacked[:, size_in:].reshape(group_size, SERVER_LAYERS, rows_down, D)
    whole_down = whole_down.transpose(1, 0, 2, 3).reshape(SERVER_LAYERS, FF, D)
    for layer in range(SERVER_LAYERS):
        weights_in.append(whole_in[layer])
        weights_down.append(whole_down[layer])
    class_shard = lax.dynamic_index_in_dim(classifier, shard_here, 0, keepdims=False)

    def loss_of(cut_rows, list_in, list_down, class_weights):
        return server_loss(cut_rows, slot_hot, list_in, list_down, class_weights)

    total_loss, server_back, per_loss = jax.vjp(
        loss_of, compact, tuple(weights_in), tuple(weights_down), class_shard, has_aux=True
    )
    grad_cut, grad_in, grad_down, grad_class = server_back(jnp.ones((), jnp.float32))
    returning = jnp.dot(
        selector.T, grad_cut.reshape(capacity, piece_rows * D), preferred_element_type=jnp.float32
    )
    returning = returning.astype(jnp.bfloat16).reshape(members, piece_rows, D)
    returned = lax.all_to_all(returning, "client", split_axis=0, concat_axis=0, tiled=True)
    own_grads = lax.dynamic_slice_in_dim(returned, own_shard * group_size, group_size, 0)
    own_grads = own_grads.reshape(IMG * TOK, D)
    client_parts = client_back(own_grads)
    summed = lax.psum_scatter(
        tuple((part_grad.astype(jnp.float32) for part_grad in client_parts)),
        "client",
        scatter_dimension=1,
        tiled=True,
    )
    blocks_in = (
        jnp.stack(grad_in)
        .astype(jnp.float32)
        .reshape(SERVER_LAYERS, group_size, rows_in * width_all)
    )
    blocks_in = blocks_in.transpose(1, 0, 2).reshape(group_size, -1)
    blocks_down = (
        jnp.stack(grad_down).astype(jnp.float32).reshape(SERVER_LAYERS, group_size, rows_down * D)
    )
    blocks_down = blocks_down.transpose(1, 0, 2).reshape(group_size, -1)
    blocks_class = grad_class.astype(jnp.float32).reshape(group_size, rows_in * CLASSES)
    blocks = jnp.concatenate([blocks_in, blocks_down, blocks_class], 1)
    order_bits = list(range(group_bits - 1, -1, -1))
    own_sum = reduce_group(blocks, group_bits, rank_in_group, order_bits)
    size_in = SERVER_LAYERS * rows_in * width_all
    size_down = SERVER_LAYERS * rows_down * D
    grad_server_in = own_sum[:size_in].reshape(SERVER_LAYERS, rows_in, width_all)
    grad_server_down = own_sum[size_in : size_in + size_down].reshape(SERVER_LAYERS, rows_down, D)
    grad_classifier = own_sum[size_in + size_down :].reshape(rows_in, CLASSES)
    return (
        per_loss.reshape(1, -1),
        summed[0],
        summed[1],
        summed[2],
        summed[3],
        grad_server_in,
        grad_server_down,
        grad_classifier,
    )


def solution(mesh):
    in_specs = (
        P("client", None),
        P(),
        P(),
        P(),
        P(),
        P(),
        P(),
        P(None, "client", None),
        P(None, "client", None),
        P(),
    )
    out_specs = (
        P("client", None),
        P(None, "client"),
        P(None, "client"),
        P(None, "client"),
        P(None, "client"),
        P(None, "client", None),
        P(None, "client", None),
        P("client", None),
    )
    return jax.shard_map(
        per_device, mesh=mesh, in_specs=in_specs, out_specs=out_specs, check_vma=False
    )
```

profile of v0, /device:TPU:15, one launch (start us, length us, event | category | flops | bytes accessed | tf_op | source)
XLA Modules:
  0.0 712.9 jit_solution(912819160223898887)
XLA Ops:
  23.3 6.5 all-to-all-start
  29.8 3.1 reshape.608
  32.9 2.3 copy.145
  35.3 10.4 %pad_maximum_fusion.1 = bf16[1769472]{0:T(1024)(128)(2,1)S(1)} fusion(bf16[589824]{0:T(1024)(128)(2,1)S(1)} %copy-done.16, bf16[1179648]{0:T(1024)(128)(2,1)S(1)} %bitcast.330), kind=kLoop, calls=%fused_computation.9 | loop fusion | flops 7077888 | bytes 7077888 | tf_op jit(solution)/shard_map/concatenate | solution.py:185
  45.7 41.6 %broadcast_in_dim.147 = bf16[1,1769472]{1,0:T(2,128)(2,1)} reshape(bf16[1769472]{0:T(1024)(128)(2,1)S(1)} %pad_maximum_fusion.1) | data formatting | bytes 7077888 | tf_op jit(solution)/shard_map/broadcast_in_dim | solution.py:111
  104.0 2.0 multiply_convert_fusion.3
  108.8 33.0 %broadcast_select_fusion = bf16[2,1769472]{1,0:T(2,128)(2,1)S(1)} fusion(pred[]{:T(512)S(6)} %eq.90, bf16[1,1769472]{1,0:T(2,128)(2,1)} %collective-permute-done, bf16[1,1769472]{1,0:T(2,128)(2,1)} %broadcast_in_dim.147), kind=kLoop, calls=%fused_computation.3 | loop fusion | flops 31850496 | bytes 14155777 | tf_op jit(solution)/shard_map/jit(_where)/select_n | solution.py:115
  141.8 3.3 slice.126
  145.2 3.4 slice.118
  154.4 2.0 fusion.81
  161.7 2.0 copy.147
  169.8 3.2 multiply_convert_fusion.1
  180.2 2.1 convert_element_type.403
  185.4 2.1 multiply_convert_fusion
  199.3 2.2 reshape.617
  201.5 2.1 convolution_bitcast_fusion.5
  203.8 1.9 multiply_reduce_fusion.1
  210.3 2.8 reshape.618
  213.2 2.0 convolution_convert_fusion.20
  231.8 3.3 reshape.622
  249.2 4.9 stack.19
  254.1 1.9 fusion.147
  267.4 2.7 pad_add_fusion.1
  270.1 4.8 stack.18
  277.0 5.6 all-to-all-start.1
  282.7 6.4 pad_maximum_fusion.2
  289.1 8.0 %pad_maximum_fusion = bf16[2,2,589824]{2,1,0:T(2,128)(2,1)} fusion(bf16[1,2,589824]{2,1,0:T(2,128)(2,1)S(1)} %copy-done.7, bf16[1,2,589824]{2,1,0:T(2,128)(2,1)S(1)} %copy-done.8), kind=kLoop, calls=%fused_computation.8 | loop fusion | flops 2359296 | bytes 9437184 | tf_op jit(solution)/shard_map/stack | solution.py:218
  297.1 56.1 %maximum_convert_fusion = f32[2,1771392]{1,0:T(2,128)S(1)} fusion(bf16[2,1920]{1,0:T(2,128)(2,1)S(1)} %copy-done.93, bf16[2,589824]{1,0:T(2,128)(2,1)} %bitcast.329, bf16[2,1179648]{1,0:T(2,128)(2,1)} %bitcast.326), kind=kLoop, calls=%fused_computation.4 | loop fusion | flops 21256704 | bytes 21256704 | tf_op jit(solution)/shard_map/concatenate | solution.py:228
  353.2 7.6 %dynamic-slice_convert_fusion = bf16[1,1771392]{1,0:T(2,128)(2,1)} fusion(f32[2,1771392]{1,0:T(2,128)S(1)} %maximum_convert_fusion, s32[]{:T(128)S(6)} %select_n.89), kind=kLoop, calls=%fused_computation.6 | loop fusion | bytes 7085572 | tf_op jit(solution)/shard_map/convert_element_type | solution.py:130
  364.2 1.9 fusion.2
  366.2 63.2 %fusion = f32[1536,16]{0,1:T(8,128)S(1)} fusion(f32[1536,384]{0,1:T(8,128)} %fusion.2), kind=kCustom, calls=%all-reduce-scatter | all-reduce-scatter fusion | flops 786433 | bytes 2457600
  432.0 11.6 %collective-permute-start.7 = (f32[1536,16]{0,1:T(8,128)S(1)}, f32[1536,16]{0,1:T(8,128)}, u32[]{:S(2)}, u32[]{:S(2)}) collective-permute-start(f32[1536,16]{0,1:T(8,128)S(1)} %fusion), channel_id=1, source_target_pairs={{0,6},{1,7},{2,8},{3,9},{4,10},{5,11},{6,12},{7,13},{8,14},{9,15},... | collective-permute-start | bytes 294920
  443.6 2.1 collective-permute-start.6
  458.9 4.6 collective-permute-start.9
  464.8 2.8 add_convert_fusion
  467.5 6.1 copy.141
  473.6 45.3 %all-reduce.19 = f32[16,384]{1,0:T(8,128)S(1)} all-reduce(bf16[16,384]{1,0:T(8,128)(2,1)S(1)} %get-tuple-element.42), channel_id=3, replica_groups=mesh['client'=32] {'client'}, use_global_device_ids=true, to_apply=%region_46.47.clone | all-reduce | flops 6144 | bytes 36864
  520.9 4.5 collective-permute-start.4
  525.4 3.1 collective-permute-start.3
  528.5 2.5 collective-permute-start.2
  532.4 3.8 concatenate.22
  536.8 56.4 %all-reduce.24.cloned.1.call-done = f32[192,384]{1,0:T(8,128)} async-done(((f32[192,384]{1,0:T(8,128)}), f32[192,384]{1,0:T(8,128)}) %all-reduce.24.cloned.1.call-update) | async-done | bytes 294928
  594.9 12.9 %convert_add_fusion = f32[1,1771392]{1,0:T(1,128)S(1)} fusion(bf16[1,1771392]{1,0:T(2,128)(2,1)} %collective-permute-done.1, f32[2,1771392]{1,0:T(2,128)} %copy-done.1, s32[]{:T(128)S(6)} %select_n.88), kind=kLoop, calls=%fused_computation.5 | loop fusion | flops 3542784 | bytes 17713924 | tf_op jit(solution)/shard_map/add | solution.py:130
  607.8 2.9 copy-done.2
  611.6 52.0 %slice_reduce_fusion = f32[1179648]{0:T(1024)} fusion(f32[1,1771392]{1,0:T(1,128)} %copy-done.2), kind=kLoop, calls=%fused_computation.7 | loop fusion | bytes 9437184 | tf_op jit(solution)/shard_map/slice | solution.py:233
  663.6 5.8 reshape.633
  669.4 25.4 %slice_reduce_fusion.1 = f32[589824]{0:T(1024)S(1)} fusion(f32[1,1771392]{1,0:T(1,128)} %copy-done.2), kind=kLoop, calls=%fused_computation.26 | loop fusion | bytes 4718592 | tf_op jit(solution)/shard_map/slice | solution.py:234
  696.5 9.3 %reduce-scatter.8.cloned.1.call-done = f32[96,384]{1,0:T(8,128)} async-done(((f32[3072,384]{1,0:T(8,128)}), f32[96,384]{1,0:T(8,128)}) %reduce-scatter.8.cloned.1.call-update) | async-done | bytes 147472
  (466 shorter events, 150.0 us)
Async XLA Ops:
  7.2 14.3 %copy-start = (bf16[1536,384]{1,0:T(8,128)(2,1)S(1)}, bf16[1536,384]{1,0:T(8,128)(2,1)}, u32[]{:S(2)}) copy-start(bf16[1536,384]{1,0:T(8,128)(2,1)} %param.16) | copy-start | bytes 3538948
  9.9 7.0 copy-start.38
  11.2 77.2 %copy-start.96 = (f32[128]{0:T(128)}, f32[128]{0:T(128)S(1)}, u32[]{:S(2)}) copy-start(f32[128]{0:T(128)S(1)} %broadcast_multiply_fusion.6) | copy-start | bytes 1540
  15.8 78.3 %copy-start.77 = (f32[8,6,16]{2,1,0:T(8,128)}, f32[8,6,16]{2,1,0:T(8,128)S(1)}, u32[]{:S(2)}) copy-start(f32[8,6,16]{2,1,0:T(8,128)S(1)} %fusion.73) | copy-start | bytes 9220
  23.3 71.5 %all-to-all-start = ((bf16[32,64,384]{2,1,0:T(8,128)(2,1)}), bf16[32,64,384]{2,1,0:T(8,128)(2,1)S(1)}, u32[]{:S(2)}, u32[]{:S(2)}) async-start(bf16[32,64,384]{2,1,0:T(8,128)(2,1)} %bitcast_select_fusion), calls=%async_computation | async-start | bytes 3145728 | tf_op jit(solution)/shard_map/all_to_all | solution.py:174
  45.6 44.4 %copy-start.109 = (s32[256]{0:T(256)S(1)}, s32[256]{0:T(256)}, u32[]{:S(2)}) copy-start(s32[256]{0:T(256)} %param.11) | copy-start | bytes 3076
  45.6 44.6 %copy-start.114 = (s32[32,1]{0,1:T(1,128)S(1)}, s32[32,1]{0,1:T(1,128)}, u32[]{:S(2)}) copy-start(s32[32,1]{0,1:T(1,128)} %param.12) | copy-start | bytes 388
  87.3 21.5 %collective-permute-start = (bf16[1,1769472]{1,0:T(2,128)(2,1)}, bf16[1,1769472]{1,0:T(2,128)(2,1)}, u32[]{:S(2)}, u32[]{:S(2)}) collective-permute-start(bf16[1,1769472]{1,0:T(2,128)(2,1)} %broadcast_in_dim.147), channel_id=1, source_target_pairs={{0,1},{1,0},{2,3},{3,2},{4,5},{5,4},{6,7},{7,6},{8,9},{9,8},{10,11... | collective-permute-start | bytes 10616840 | tf_op jit(solution)/shard_map/ppermute | solution.py:29
  90.4 5.6 copy-start.104
  90.4 5.6 copy-start.106
  177.1 5.2 copy-start.60
  185.2 12.0 %copy-start.64 = (f32[16,16]{1,0:T(8,128)}, f32[16,16]{1,0:T(8,128)S(1)}, u32[]{:S(2)}) copy-start(f32[16,16]{1,0:T(8,128)S(1)} %fusion.104) | copy-start | bytes 3076
  191.1 6.1 copy-start.50
  231.8 11.2 %copy-start.19 = (bf16[1536,384]{1,0:T(8,128)(2,1)S(1)}, bf16[1536,384]{1,0:T(8,128)(2,1)}, u32[]{:S(2)}) copy-start(bf16[1536,384]{1,0:T(8,128)(2,1)} %fusion.141) | copy-start | bytes 3538948
  249.2 6.8 copy-start.20
  254.1 8.8 %copy-start.76 = (f32[16,16]{1,0:T(8,128)S(1)}, f32[16,16]{1,0:T(8,128)}, u32[]{:S(2)}) copy-start(f32[16,16]{1,0:T(8,128)} %copy-done.75) | copy-start | bytes 3076
  257.4 10.0 %copy-start.22 = (bf16[384,1536]{1,0:T(8,128)(2,1)S(1)}, bf16[384,1536]{1,0:T(8,128)(2,1)}, u32[]{:S(2)}) copy-start(bf16[384,1536]{1,0:T(8,128)(2,1)} %fusion.144) | copy-start | bytes 3538948
  277.0 5.7 copy-start.24
  277.0 84.8 %all-to-all-start.1 = ((bf16[32,64,384]{2,1,0:T(8,128)(2,1)}), bf16[32,64,384]{2,1,0:T(8,128)(2,1)}, u32[]{:S(2)}, u32[]{:S(2)}) async-start(bf16[32,64,384]{2,1,0:T(8,128)(2,1)} %bitcast.137), calls=%async_computation.1 | async-start | bytes 3145728 | tf_op jit(solution)/shard_map/all_to_all | solution.py:207
  282.6 310.6 %all-reduce.24.cloned.1.call-start = ((), (), s32[]{:S(2)}) async-start(), calls=%async_computation.4 | async-start | bytes 589824
  282.6 6.4 copy-start.7
  282.7 6.4 copy-start.8
  289.1 8.0 %copy-start.93 = (bf16[2,1920]{1,0:T(2,128)(2,1)S(1)}, bf16[2,1920]{1,0:T(2,128)(2,1)}, u32[]{:S(2)}) copy-start(bf16[2,1920]{1,0:T(2,128)(2,1)} %reshape.632) | copy-start | bytes 23044
  353.2 7.7 %copy-start.1 = (f32[2,1771392]{1,0:T(2,128)}, f32[2,1771392]{1,0:T(2,128)S(1)}, u32[]{:S(2)}) copy-start(f32[2,1771392]{1,0:T(2,128)S(1)} %maximum_convert_fusion) | copy-start | bytes 42513412
  353.2 8.1 %copy-start.99 = (f32[16]{0:T(128)S(1)}, f32[16]{0:T(128)}, u32[]{:S(2)}) copy-start(f32[16]{0:T(128)} %reduce_sum.472) | copy-start | bytes 196
  353.2 8.1 %copy-start.101 = (f32[16]{0:T(128)S(1)}, f32[16]{0:T(128)}, u32[]{:S(2)}) copy-start(f32[16]{0:T(128)} %copy-done.100) | copy-start | bytes 196
  353.2 8.1 %copy-start.108 = (f32[16]{0:T(128)S(1)}, f32[16]{0:T(128)}, u32[]{:S(2)}) copy-start(f32[16]{0:T(128)} %get-tuple-element.41) | copy-start | bytes 196
  353.2 8.1 %copy-start.113 = (f32[16]{0:T(128)S(1)}, f32[16]{0:T(128)}, u32[]{:S(2)}) copy-start(f32[16]{0:T(128)} %copy-done.112) | copy-start | bytes 196
  353.2 9.5 %copy-start.33 = (f32[128,1536]{1,0:T(8,128)S(1)}, f32[128,1536]{1,0:T(8,128)}, u32[]{:S(2)}) copy-start(f32[128,1536]{1,0:T(8,128)} %copy-done.32) | copy-start | bytes 2359300
  360.9 234.0 %collective-permute-start.1 = (bf16[1,1771392]{1,0:T(2,128)(2,1)}, bf16[1,1771392]{1,0:T(2,128)(2,1)}, u32[]{:S(2)}, u32[]{:S(2)}) collective-permute-start(bf16[1,1771392]{1,0:T(2,128)(2,1)} %dynamic-slice_convert_fusion), channel_id=1, source_target_pairs={{0,1},{1,0},{2,3},{3,2},{4,5},{5,4},{6,7},{7,6},{8,9},{9,8},{10,11... | collective-permute-start | bytes 10628360 | tf_op jit(solution)/shard_map/ppermute | solution.py:29
  366.2 81.5 %copy-start.68 = (f32[8,16]{1,0:T(8,128)S(1)}, f32[8,16]{1,0:T(8,128)}, u32[]{:S(2)}) copy-start(f32[8,16]{1,0:T(8,128)} %copy-done.67) | copy-start | bytes 1540
  366.2 81.7 %copy-start.92 = (f32[8,16]{1,0:T(8,128)S(1)}, f32[8,16]{1,0:T(8,128)}, u32[]{:S(2)}) copy-start(f32[8,16]{1,0:T(8,128)} %copy-done.91) | copy-start | bytes 1540
  366.2 81.7 %copy-start.89 = (f32[8,16]{1,0:T(8,128)S(1)}, f32[8,16]{1,0:T(8,128)}, u32[]{:S(2)}) copy-start(f32[8,16]{1,0:T(8,128)} %copy-done.88) | copy-start | bytes 1540
  429.4 20.9 %copy-start.18 = (f32[8,16,3,6,64]{4,1,3,2,0:T(8,128)S(1)}, f32[8,16,3,6,64]{4,1,3,2,0:T(8,128)}, u32[]{:S(2)}) copy-start(f32[8,16,3,6,64]{4,1,3,2,0:T(8,128)} %copy-done.17) | copy-start | bytes 1769476
  429.4 20.9 %copy-start.30 = (f32[8,6,16,16]{2,3,1,0:T(8,128)S(1)}, f32[8,6,16,16]{2,3,1,0:T(8,128)}, u32[]{:S(2)}) copy-start(f32[8,6,16,16]{2,3,1,0:T(8,128)} %copy-done.29) | copy-start | bytes 147460
  430.1 90.8 %collective-permute-start.8 = (f32[1536,16]{0,1:T(8,128)S(1)}, f32[1536,16]{0,1:T(8,128)}, u32[]{:S(2)}, u32[]{:S(2)}) collective-permute-start(f32[1536,16]{0,1:T(8,128)S(1)} %fusion), channel_id=1, source_target_pairs={{0,7},{1,8},{2,9},{3,10},{4,11},{5,12},{6,13},{7,14},{8,15},{9,16}... | collective-permute-start | bytes 294920
  432.0 93.4 %collective-permute-start.7 = (f32[1536,16]{0,1:T(8,128)S(1)}, f32[1536,16]{0,1:T(8,128)}, u32[]{:S(2)}, u32[]{:S(2)}) collective-permute-start(f32[1536,16]{0,1:T(8,128)S(1)} %fusion), channel_id=1, source_target_pairs={{0,6},{1,7},{2,8},{3,9},{4,10},{5,11},{6,12},{7,13},{8,14},{9,15},... | collective-permute-start | bytes 294920
  443.6 84.9 %collective-permute-start.6 = (f32[1536,16]{0,1:T(8,128)S(1)}, f32[1536,16]{0,1:T(8,128)}, u32[]{:S(2)}, u32[]{:S(2)}) collective-permute-start(f32[1536,16]{0,1:T(8,128)S(1)} %fusion), channel_id=1, source_target_pairs={{0,5},{1,6},{2,7},{3,8},{4,9},{5,10},{6,11},{7,12},{8,13},{9,14},{... | collective-permute-start | bytes 294920
  455.0 8.5 %copy-start.48 = (bf16[128,384]{1,0:T(8,128)(2,1)S(1)}, bf16[128,384]{1,0:T(8,128)(2,1)}, u32[]{:S(2)}) copy-start(bf16[128,384]{1,0:T(8,128)(2,1)} %convert_element_type.390) | copy-start | bytes 294916
  455.1 8.8 %copy-start.41 = (bf16[128,384]{1,0:T(8,128)(2,1)S(1)}, bf16[128,384]{1,0:T(8,128)(2,1)}, u32[]{:S(2)}) copy-start(bf16[128,384]{1,0:T(8,128)(2,1)} %copy-done.40) | copy-start | bytes 294916
  455.6 8.7 %copy-start.43 = (bf16[8,16,384]{2,1,0:T(8,128)(2,1)S(1)}, bf16[8,16,384]{2,1,0:T(8,128)(2,1)}, u32[]{:S(2)}) copy-start(bf16[8,16,384]{2,1,0:T(8,128)(2,1)} %copy-done.42) | copy-start | bytes 294916
  455.6 8.7 %copy-start.49 = (bf16[128,1536]{1,0:T(8,128)(2,1)S(1)}, bf16[128,1536]{1,0:T(8,128)(2,1)}, u32[]{:S(2)}) copy-start(bf16[128,1536]{1,0:T(8,128)(2,1)} %fusion.41) | copy-start | bytes 1179652
  458.8 246.9 %reduce-scatter.8.cloned.1.call-start = ((), (), s32[]{:S(2)}) async-start(), calls=%async_computation.3 | async-start | bytes 4866048
  458.9 60.0 %collective-permute-start.9 = (f32[1536,12]{0,1:T(8,128)S(1)}, f32[1536,12]{0,1:T(8,128)S(1)}, u32[]{:S(2)}, u32[]{:S(2)}) collective-permute-start(f32[1536,12]{0,1:T(8,128)S(1)} %copy-done.79), channel_id=1, source_target_pairs={{0,8},{1,9},{2,10},{3,11},{4,12},{5,13},{6,14},{7,15},{8,16},{9,17... | collective-permute-start | bytes 221192
  518.9 12.8 %collective-permute-start.5 = (f32[1536,16]{0,1:T(8,128)S(1)}, f32[1536,16]{0,1:T(8,128)S(1)}, u32[]{:S(2)}, u32[]{:S(2)}) collective-permute-start(f32[1536,16]{0,1:T(8,128)S(1)} %fusion), channel_id=1, source_target_pairs={{0,4},{1,5},{2,6},{3,7},{4,8},{5,9},{6,10},{7,11},{8,12},{9,13},{1... | collective-permute-start | bytes 294920
  520.9 10.8 %collective-permute-start.4 = (f32[1536,16]{0,1:T(8,128)S(1)}, f32[1536,16]{0,1:T(8,128)S(1)}, u32[]{:S(2)}, u32[]{:S(2)}) collective-permute-start(f32[1536,16]{0,1:T(8,128)S(1)} %fusion), channel_id=1, source_target_pairs={{0,3},{1,4},{2,5},{3,6},{4,7},{5,8},{6,9},{7,10},{8,11},{9,12},{10... | collective-permute-start | bytes 294920
  525.4 6.4 collective-permute-start.3
  528.5 3.9 collective-permute-start.2
  (82 other events, 195.0 us)
Sparse Core Ops, SparseCore 0:
  458.9 134.2 all-reduce.23
  599.2 106.4 reduce-scatter.7
where the time goes:
time: 723 us; the launch traced here: 713 us
  local copies, waits for them, and re-layouts  242 us (33%)
  other arithmetic  157 us (22%)
  blocking collectives  109 us (15%)
  matrix products  75.8 us (10%)
  waiting for transfers between devices  66.4 us (9%)
  starting transfers between devices  45.3 us (6%)
  between operations  17.3 us (2%)
    unnamed x2, blocking collectives  109 us
    unnamed x12, waiting for transfers between devices  66.4 us
    concatenate x1, other arithmetic, per_device(): blocks = jnp.concatenate([blocks_in, blocks_down, blocks_class], 1)  56.1 us
    slice x1, local copies, waits for them, and re-layouts, per_device(): own_sum[:size_in].reshape(SERVER_LAYERS, rows_in, width_all)  52 us
    broadcast_in_dim x1, local copies, waits for them, and re-layouts, gather_group(): stacked = flat_rows[None]  41.6 us
    select_n x1, other arithmetic, gather_group(): jnp.where(upper_half == 0, jnp.concatenate([stacked, partner], 0), jnp.co...  33 us
    unnamed x249, local copies, waits for them, and re-layouts  32.7 us
    unnamed x10, starting transfers between devices  32.3 us
  transfers between devices with their start and end apart: 14, of which 4 were waited for; matrix products, arithmetic and copies ran while one was open for 49% of the time, Pallas kernels for 0%

commit v1 on v0

v1 whole, which is shorter than its diff:
```python
import functools
import math

import jax
import jax.numpy as jnp
from jax import lax
from jax.experimental import pallas as pl
from jax.experimental.pallas import tpu as pltpu
from jax.sharding import PartitionSpec as P

HEADS = 6
TOK = 16
IMG = 8
SHARDS = 16
SLOTS = 2
EPSILON = 1e-06
LANES = 128
PAD = 16
BF = jnp.bfloat16
F32 = jnp.float32
HIGH = lax.Precision.HIGHEST
GELU_C = math.sqrt(2.0 / math.pi)
VMEM_LIMIT = 60 * 1024 * 1024
MESH = pl.DeviceIdType.MESH


def mm(a, b, precision=None):
    return lax.dot_general(
        a, b, (((1,), (0,)), ((), ())), precision=precision, preferred_element_type=F32
    )


def mm_nt(a, b, precision=None):
    return lax.dot_general(
        a, b, (((1,), (1,)), ((), ())), precision=precision, preferred_element_type=F32
    )


def mm_tn(a, b):
    return lax.dot_general(a, b, (((0,), (0,)), ((), ())), preferred_element_type=F32)


def norm(v):
    centre = v - jnp.mean(v, axis=-1, keepdims=True)
    scale = lax.rsqrt(jnp.mean(centre * centre, axis=-1, keepdims=True) + EPSILON)
    return centre * scale, scale


def norm_back(normed, scale, grad):
    return scale * (
        grad
        - jnp.mean(grad, axis=-1, keepdims=True)
        - normed * jnp.mean(grad * normed, axis=-1, keepdims=True)
    )


def gelu(v):
    t = jnp.tanh(GELU_C * (v + 0.044715 * (v * v * v)))
    return 0.5 * v * (1.0 + t)


def gelu_both(v):
    sq = v * v
    t = jnp.tanh(GELU_C * (v + 0.044715 * (sq * v)))
    value = 0.5 * v * (1.0 + t)
    slope = 0.5 * (1.0 + t) + 0.5 * v * (1.0 - t * t) * (GELU_C * (1.0 + 0.134145 * sq))
    return value, slope


def image_mask():
    row = lax.broadcasted_iota(jnp.int32, (LANES, LANES), 0)
    col = lax.broadcasted_iota(jnp.int32, (LANES, LANES), 1)
    return row // TOK == col // TOK


def lane_masks(head_dim):
    lane = lax.broadcasted_iota(jnp.int32, (LANES, LANES), 1)
    return [lane // head_dim == h for h in range(LANES // head_dim)]


def attend(qkv_ref, probs_ref, att_ref, width):
    rows = qkv_ref.shape[0]
    head_dim = width // HEADS
    per = LANES // head_dim
    inside = image_mask()
    keeps = lane_masks(head_dim)
    for group in range(rows // LANES):
        r = slice(group * LANES, (group + 1) * LANES)
        for pair in range(width // LANES):
            lo = pair * LANES
            q = qkv_ref[r, lo : lo + LANES]
            k = qkv_ref[r, width + lo : width + lo + LANES]
            v = qkv_ref[r, 2 * width + lo : 2 * width + lo + LANES]
            out = jnp.zeros((LANES, LANES), F32)
            for h in range(per):
                s = mm_nt(jnp.where(keeps[h], q, 0.0), k, HIGH) * (1.0 / math.sqrt(head_dim))
                s = jnp.where(inside, s, -1e30)
                e = jnp.exp(s - jnp.max(s, axis=-1, keepdims=True))
                p = (e / jnp.sum(e, axis=-1, keepdims=True)).astype(BF)
                probs_ref[group * HEADS + pair * per + h] = p
                out = out + mm(p, jnp.where(keeps[h], v, 0.0).astype(BF))
            att_ref[r, lo : lo + LANES] = out.astype(BF)


def attend_back(grad, qkv_ref, probs_ref, dqkv_ref, width):
    rows = qkv_ref.shape[0]
    head_dim = width // HEADS
    per = LANES // head_dim
    keeps = lane_masks(head_dim)
    for group in range(rows // LANES):
        r = slice(group * LANES, (group + 1) * LANES)
        for pair in range(width // LANES):
            lo = pair * LANES
            q = qkv_ref[r, lo : lo + LANES]
            k = qkv_ref[r, width + lo : width + lo + LANES]
            v = qkv_ref[r, 2 * width + lo : 2 * width + lo + LANES].astype(BF)
            go = grad[r, lo : lo + LANES]
            dq = jnp.zeros((LANES, LANES), F32)
            dk = jnp.zeros((LANES, LANES), F32)
            dv = jnp.zeros((LANES, LANES), F32)
            for h in range(per):
                p = probs_ref[group * HEADS + pair * per + h]
                goh = jnp.where(keeps[h], go, 0.0).astype(BF)
                dp = mm_nt(goh, v)
                dv = dv + mm_tn(p, goh)
                pf = p.astype(F32)
                ds = pf * (dp - jnp.sum(pf * dp, axis=-1, keepdims=True))
                ds = (ds * (1.0 / math.sqrt(head_dim))).astype(BF)
                dq = dq + mm(ds, jnp.where(keeps[h], k, 0.0).astype(BF))
                dk = dk + mm_tn(ds, jnp.where(keeps[h], q, 0.0).astype(BF))
            dqkv_ref[r, lo : lo + LANES] = dq.astype(BF)
            dqkv_ref[r, width + lo : width + lo + LANES] = dk.astype(BF)
            dqkv_ref[r, 2 * width + lo : 2 * width + lo + LANES] = dv.astype(BF)


def block_forward(x, w_ref, d_ref, qkv_ref, probs_ref, att_ref, mid_ref, pre_ref):
    width = x.shape[1]
    u = norm(x)[0].astype(BF)
    qkv_ref[...] = mm(u, w_ref[:, : 3 * width])
    attend(qkv_ref, probs_ref, att_ref, width)
    y = x + mm(att_ref[...], w_ref[:, 3 * width : 4 * width])
    mid_ref[...] = y
    u = norm(y)[0].astype(BF)
    pre_ref[...] = mm(u, w_ref[:, 4 * width :])
    h = gelu(pre_ref[...]).astype(BF)
    return y + mm(h, d_ref[...])


def block_backward(
    g, x, w_ref, d_ref, qkv_ref, probs_ref, att_ref, mid_ref, pre_ref, dqkv_ref, put_in, put_down
):
    width = x.shape[1]
    gb = g.astype(BF)
    h, slope = gelu_both(pre_ref[...])
    put_down(h.astype(BF), gb)
    dpre = (mm_nt(gb, d_ref[...]) * slope).astype(BF)
    y = mid_ref[...]
    u, scale = norm(y)
    put_in(4 * width, u.astype(BF), dpre)
    dy = g + norm_back(u, scale, mm_nt(dpre, w_ref[:, 4 * width :]))
    gb = dy.astype(BF)
    put_in(3 * width, att_ref[...], gb)
    attend_back(
        mm_nt(gb, w_ref[:, 3 * width : 4 * width]), qkv_ref, probs_ref, dqkv_ref, width
    )
    u, scale = norm(x)
    dqkv = dqkv_ref[...]
    put_in(0, u.astype(BF), dqkv)
    return dy + norm_back(u, scale, mm_nt(dqkv, w_ref[:, : 3 * width]))


def client_forward_kernel(
    patch_ref, embed_ref, pos_ref, w_ref, d_ref,
    cut_ref, x_ref, qkv_ref, probs_ref, att_ref, mid_ref, pre_ref,
):
    rows = patch_ref.shape[0]
    x = mm(patch_ref[...], embed_ref[...])
    pos = pos_ref[...].astype(F32)
    x = x + jnp.concatenate([pos] * (rows // TOK), axis=0)
    x_ref[...] = x
    cut_ref[...] = block_forward(
        x, w_ref, d_ref, qkv_ref, probs_ref, att_ref, mid_ref, pre_ref
    ).astype(BF)


def client_backward_kernel(
    n, group,
    assign_ref, back_ref, patch_ref, w_ref, d_ref,
    x_ref, qkv_ref, probs_ref, att_ref, mid_ref, pre_ref,
    pack_ref,
    got, dqkv_ref, sem,
):
    me = lax.axis_index("client")
    shard = assign_ref[me]
    copy = pltpu.make_async_copy(back_ref.at[pl.ds(shard * group, group)], got, sem)
    copy.start()
    rows, width = x_ref.shape
    ff = d_ref.shape[0]
    r_in = w_ref.shape[1] // n
    cols = width // n
    src = lax.broadcasted_iota(jnp.int32, (width, n * PAD), 0)
    dst = lax.broadcasted_iota(jnp.int32, (width, n * PAD), 1)
    place = ((dst // PAD == src // cols) & (dst % PAD == src % cols)).astype(F32).astype(BF)
    tok = (
        lax.broadcasted_iota(jnp.int32, (rows, LANES), 0) % TOK
        == lax.broadcasted_iota(jnp.int32, (rows, LANES), 1)
    ).astype(F32).astype(BF)
    copy.wait()
    g = got[...].astype(F32).reshape(rows, width)
    per_dev = w_ref.shape[1] // n

    def put_in(start, lhs, rhs):
        for c in range(0, rhs.shape[1], width):
            part = mm_tn(rhs[:, c : c + width], lhs)
            j = (start + c) // per_dev
            pack_ref[j : j + width // per_dev, :per_dev, :] = part.reshape(
                width // per_dev, per_dev, width
            ).astype(BF)

    def put_down(h, gb):
        spread = mm(gb, place).astype(BF)
        for q in range(ff // width):
            part = mm_tn(spread, h[:, q * width : (q + 1) * width])
            lo = r_in + q * PAD
            pack_ref[:, lo : lo + PAD, :] = part.reshape(n, PAD, width).astype(BF)

    dx = block_backward(
        g, x_ref[...], w_ref, d_ref, qkv_ref, probs_ref, att_ref, mid_ref, pre_ref,
        dqkv_ref, put_in, put_down,
    )
    spread = mm(dx.astype(BF), place).astype(BF)
    lo = r_in + (ff // width) * PAD
    patch = patch_ref.shape[1]
    pack_ref[:, lo : lo + PAD, :patch] = mm_tn(spread, patch_ref[...]).reshape(
        n, PAD, patch
    ).astype(BF)
    pack_ref[:, lo : lo + PAD, width - LANES :] = mm_tn(spread, tok).reshape(
        n, PAD, LANES
    ).astype(BF)


def server_kernel(
    n, group, layers, per_image, capacity, classes, *refs,
):
    assign_ref, label_ref, arrived_ref, class_ref = refs[:4]
    refs = refs[4:]
    in_pieces, refs = refs[:group], refs[group:]
    down_pieces, refs = refs[:group], refs[group:]
    loss_ref, back_ref, gclass_ref = refs[:3]
    refs = refs[3:]
    gin_out, refs = refs[:group], refs[group:]
    gdown_out, refs = refs[:group], refs[group:]
    (
        wbuf, dbuf, gin, gdown, xs, qkv, probs, att, mid, pre, dqkv, gcur, cut,
        slot_ref, w_sem, g_sem, slot_sem,
    ) = refs
    me = lax.axis_index("client")
    rank = me % group
    shard = me // group
    rows_in = in_pieces[0].shape[1]
    rows_down = down_pieces[0].shape[1]
    piece = arrived_ref.shape[1]

    def weight_copies(layer):
        made = []
        for i in range(group):
            who = rank ^ i
            made.append(pltpu.make_async_copy(
                in_pieces[i].at[layer],
                wbuf.at[layer, pl.ds(pl.multiple_of(who * rows_in, rows_in), rows_in)],
                w_sem.at[layer, 2 * i],
            ))
            made.append(pltpu.make_async_copy(
                down_pieces[i].at[layer],
                dbuf.at[layer, pl.ds(pl.multiple_of(who * rows_down, rows_down), rows_down)],
                w_sem.at[layer, 2 * i + 1],
            ))
        return made

    def grad_copies(layer):
        made = []
        for i in range(group):
            who = rank ^ i
            made.append(pltpu.make_async_copy(
                gin.at[layer, pl.ds(pl.multiple_of(who * rows_in, rows_in), rows_in)],
                gin_out[i].at[layer],
                g_sem.at[layer, 2 * i],
            ))
            made.append(pltpu.make_async_copy(
                gdown.at[layer, pl.ds(pl.multiple_of(who * rows_down, rows_down), rows_down)],
                gdown_out[i].at[layer],
                g_sem.at[layer, 2 * i + 1],
            ))
        return made

    for layer in range(layers):
        for c in weight_copies(layer):
            c.start()

    for k in range(capacity):
        slot_ref[k] = 0

    def scan(c, count):
        hit = assign_ref[c] == shard

        @pl.when(hit)
        def _():
            slot_ref[count] = c

        return count + jnp.where(hit, 1, 0)

    filled = lax.fori_loop(0, n, scan, 0)

    def slot_in(k):
        return pltpu.make_async_copy(
            arrived_ref.at[slot_ref[k]], cut.at[pl.ds(k * piece, piece)], slot_sem.at[k]
        )

    for k in range(capacity):
        @pl.when(k < filled)
        def _():
            slot_in(k).start()

        @pl.when(k >= filled)
        def _():
            cut[k * piece : (k + 1) * piece, :] = jnp.zeros((piece, cut.shape[1]), BF)

    images = capacity * per_image
    row = lax.broadcasted_iota(jnp.int32, (images, LANES), 0)
    lane = lax.broadcasted_iota(jnp.int32, (images, LANES), 1)
    want = jnp.full((images, LANES), -1, jnp.int32)
    for k in range(capacity):
        base = slot_ref[k] * (group * per_image) + rank * per_image
        for j in range(per_image):
            lab = jnp.where(k < filled, label_ref[base + j], -1)
            want = jnp.where(row == k * per_image + j, lab, want)
    hot = (lane == want).astype(F32)
    full = (want[:, :1] >= 0).astype(F32)

    for k in range(capacity):
        @pl.when(k < filled)
        def _():
            slot_in(k).wait()

    xs[0] = cut[...].astype(F32)

    def forward(layer, carry):
        for c in weight_copies(layer):
            c.wait()
        xs[layer + 1] = block_forward(
            xs[layer], wbuf.at[layer], dbuf.at[layer], qkv.at[layer], probs.at[layer],
            att.at[layer], mid.at[layer], pre.at[layer],
        )
        return carry

    lax.fori_loop(0, layers, forward, 0)

    rows = cut.shape[0]
    pool = (
        lax.broadcasted_iota(jnp.int32, (images, rows), 1) // TOK
        == lax.broadcasted_iota(jnp.int32, (images, rows), 0)
    ).astype(F32) * (1.0 / TOK)
    unpool = (
        lax.broadcasted_iota(jnp.int32, (rows, images), 0) // TOK
        == lax.broadcasted_iota(jnp.int32, (rows, images), 1)
    ).astype(F32) * (1.0 / TOK)
    u, scale = norm(mm(pool, xs[layers], HIGH))
    pooled = u.astype(BF)
    logits = mm(pooled, class_ref[...])
    logits = jnp.where(lane < classes, logits, -1e30)
    top = jnp.max(logits, axis=-1, keepdims=True)
    e = jnp.exp(logits - top)
    total = jnp.sum(e, axis=-1, keepdims=True)
    loss = (
        jnp.log(total) + top - jnp.sum(jnp.where(lane == want, logits, 0.0), axis=-1, keepdims=True)
    ) * full
    eye = (
        lax.broadcasted_iota(jnp.int32, (images, images), 0)
        == lax.broadcasted_iota(jnp.int32, (images, images), 1)
    )
    loss_ref[...] = jnp.sum(jnp.where(eye, loss, 0.0), axis=0, keepdims=True)
    dlog = ((e / total - hot) * full).astype(BF)
    gclass_ref[...] = mm_tn(pooled, dlog).astype(BF)
    dpool = norm_back(u, scale, mm_nt(dlog, class_ref[...]))
    gcur[...] = mm(unpool, dpool, HIGH)

    def backward(i, carry):
        layer = layers - 1 - i

        def put_in(start, lhs, rhs):
            gin[layer, :, start : start + rhs.shape[1]] = mm_tn(lhs, rhs).astype(BF)

        def put_down(h, gb):
            gdown[layer] = mm_tn(h, gb).astype(BF)

        gcur[...] = block_backward(
            gcur[...], xs[layer], wbuf.at[layer], dbuf.at[layer], qkv.at[layer],
            probs.at[layer], att.at[layer], mid.at[layer], pre.at[layer], dqkv,
            put_in, put_down,
        )
        for c in grad_copies(layer):
            c.start()
        return carry

    lax.fori_loop(0, layers, backward, 0)
    cut[...] = gcur[...].astype(BF)

    def slot_out(k):
        return pltpu.make_async_copy(
            cut.at[pl.ds(k * piece, piece)], back_ref.at[slot_ref[k]], slot_sem.at[k]
        )

    for k in range(capacity):
        @pl.when(k < filled)
        def _():
            slot_out(k).start()

    for k in range(capacity):
        @pl.when(k < filled)
        def _():
            slot_out(k).wait()

    for layer in range(layers):
        for c in grad_copies(layer):
            c.wait()


def greet_all(n, me):
    barrier = pltpu.get_barrier_semaphore()

    def greet(k, carry):
        pl.semaphore_signal(
            barrier, inc=1, device_id=(lax.rem(me + k, n),), device_id_type=MESH
        )
        return carry

    lax.fori_loop(1, n, greet, 0)
    pl.semaphore_wait(barrier, n - 1)


def exchange(n, me, source, target, send_sem, recv_sem, own_sem):
    own = pltpu.make_async_copy(source(me), target.at[me], own_sem)
    own.start()

    def remote(k):
        to = lax.rem(me + k, n)
        return pltpu.make_async_remote_copy(
            src_ref=source(to), dst_ref=target.at[me], send_sem=send_sem.at[k],
            recv_sem=recv_sem.at[k], device_id=(to,), device_id_type=MESH,
        )

    def start(k, carry):
        remote(k).start()
        return carry

    def finish(k, carry):
        remote(k).wait()
        return carry

    lax.fori_loop(1, n, start, 0)
    own.wait()
    lax.fori_loop(1, n, finish, 0)


def spread_kernel(n, group, cut_ref, out_ref, send_sem, recv_sem, own_sem):
    me = lax.axis_index("client")
    greet_all(n, me)
    exchange(
        n, me, lambda to: cut_ref.at[lax.rem(to, group)], out_ref, send_sem, recv_sem, own_sem
    )


def swap_kernel(n, in_ref, out_ref, send_sem, recv_sem, own_sem):
    me = lax.axis_index("client")
    greet_all(n, me)
    exchange(n, me, lambda to: in_ref.at[to], out_ref, send_sem, recv_sem, own_sem)


def total_kernel(n, in_ref, out_ref, got, send_sem, recv_sem, own_sem):
    me = lax.axis_index("client")
    greet_all(n, me)
    exchange(n, me, lambda to: in_ref.at[to], got, send_sem, recv_sem, own_sem)
    out_ref[...] = got[0].astype(F32)

    def add(k, carry):
        out_ref[...] += got[k].astype(F32)
        return carry

    lax.fori_loop(1, n, add, 0)


def vmem():
    return pl.BlockSpec(memory_space=pltpu.VMEM)


def smem():
    return pl.BlockSpec(memory_space=pltpu.SMEM)


def hbm():
    return pl.BlockSpec(memory_space=pl.ANY)


def comm_call(kernel, out, in_spec, out_spec, scratch, n, ident, arg):
    return pl.pallas_call(
        kernel,
        out_shape=out,
        in_specs=[in_spec],
        out_specs=out_spec,
        scratch_shapes=scratch
        + [
            pltpu.SemaphoreType.DMA((n,)),
            pltpu.SemaphoreType.DMA((n,)),
            pltpu.SemaphoreType.DMA,
        ],
        compiler_params=pltpu.CompilerParams(
            collective_id=ident, has_side_effects=True, vmem_limit_bytes=VMEM_LIMIT
        ),
    )(arg)


def shape(dims, kind):
    return jax.ShapeDtypeStruct(dims, kind)


def flip(block, bit):
    n = lax.axis_size("client")
    return lax.ppermute(block, "client", [(i, i ^ (1 << bit)) for i in range(n)])


def per_device(
    patches, labels, assign, patch_embed, positions, client_in, client_down,
    server_in, server_down, classifier,
):
    n = lax.axis_size("client")
    group = n // SHARDS
    bits = group.bit_length() - 1
    me = lax.axis_index("client")
    rank = me % group
    shard = me // group
    rows = patches.shape[0]
    width = client_in.shape[0]
    cols = client_in.shape[1]
    ff = client_down.shape[0]
    layers = server_in.shape[0]
    rows_in = server_in.shape[1]
    rows_down = server_down.shape[1]
    classes = classifier.shape[2]
    piece = rows // group
    per_image = IMG // group
    capacity = SLOTS * group
    s_rows = capacity * piece
    routes = assign.reshape(n)
    params = pltpu.CompilerParams(vmem_limit_bytes=VMEM_LIMIT)

    in_pieces = [server_in]
    down_pieces = [server_down]
    for bit in range(bits):
        in_pieces = in_pieces + [flip(p, bit) for p in in_pieces]
        down_pieces = down_pieces + [flip(p, bit) for p in down_pieces]

    def kept(r):
        return [
            shape((r, 3 * width), F32),
            shape((r // LANES * HEADS, LANES, LANES), BF),
            shape((r, width), BF),
            shape((r, width), F32),
            shape((r, ff), F32),
        ]

    cut, x0, *saved = pl.pallas_call(
        client_forward_kernel,
        out_shape=[shape((rows, width), BF), shape((rows, width), F32)] + kept(rows),
        in_specs=[vmem()] * 5,
        out_specs=[vmem()] * 7,
        compiler_params=params,
    )(patches, patch_embed, positions, client_in, client_down)

    arrived = comm_call(
        functools.partial(spread_kernel, n, group),
        shape((n, piece, width), BF), vmem(), hbm(), [], n, 1,
        cut.reshape(group, piece, width),
    )

    class_shard = jnp.pad(
        lax.dynamic_index_in_dim(classifier, shard, 0, keepdims=False),
        ((0, 0), (0, LANES - classes)),
    )
    part_in = shape((layers, rows_in, cols), BF)
    part_down = shape((layers, rows_down, width), BF)
    res = pl.pallas_call(
        functools.partial(server_kernel, n, group, layers, per_image, capacity, classes),
        out_shape=[
            shape((1, capacity * per_image), F32),
            shape((n, piece, width), BF),
            shape((width, LANES), BF),
        ]
        + [part_in] * group
        + [part_down] * group,
        in_specs=[smem(), smem(), hbm(), vmem()] + [hbm()] * (2 * group),
        out_specs=[vmem(), hbm(), vmem()] + [hbm()] * (2 * group),
        scratch_shapes=[
            pltpu.VMEM((layers, width, cols), BF),
            pltpu.VMEM((layers, ff, width), BF),
            pltpu.VMEM((layers, width, cols), BF),
            pltpu.VMEM((layers, ff, width), BF),
            pltpu.VMEM((layers + 1, s_rows, width), F32),
        ]
        + [pltpu.VMEM((layers,) + s.shape, s.dtype) for s in kept(s_rows)]
        + [
            pltpu.VMEM((s_rows, 3 * width), BF),
            pltpu.VMEM((s_rows, width), F32),
            pltpu.VMEM((s_rows, width), BF),
            pltpu.SMEM((capacity,), jnp.int32),
            pltpu.SemaphoreType.DMA((layers, 2 * group)),
            pltpu.SemaphoreType.DMA((layers, 2 * group)),
            pltpu.SemaphoreType.DMA((capacity,)),
        ],
        compiler_params=params,
    )(routes, labels, arrived, class_shard, *in_pieces, *down_pieces)
    losses, back, gclass = res[:3]
    parts_in = list(res[3 : 3 + group])
    parts_down = list(res[3 + group :])

    returned = comm_call(
        functools.partial(swap_kernel, n),
        shape((n, piece, width), BF), hbm(), hbm(), [], n, 2, back,
    )

    half = group // 2
    while half:
        bit = half.bit_length() - 1
        parts_in = [
            parts_in[i].astype(F32) + flip(parts_in[i + half].astype(BF), bit).astype(F32)
            for i in range(half)
        ]
        parts_down = [
            parts_down[i].astype(F32) + flip(parts_down[i + half].astype(BF), bit).astype(F32)
            for i in range(half)
        ]
        half //= 2
    gsum = gclass.astype(F32)
    for bit in range(bits):
        gsum = gsum + flip(gsum.astype(BF), bit).astype(F32)
    grad_class = lax.dynamic_slice_in_dim(gsum, rank * rows_in, rows_in, 0)[:, :classes]

    r_in = cols // n
    pack_rows = r_in + (ff // width + 1) * PAD
    packed = pl.pallas_call(
        functools.partial(client_backward_kernel, n, group),
        out_shape=shape((n, pack_rows, width), BF),
        in_specs=[smem(), hbm()] + [vmem()] * 9,
        out_specs=vmem(),
        scratch_shapes=[
            pltpu.VMEM((group, piece, width), BF),
            pltpu.VMEM((rows, 3 * width), BF),
            pltpu.SemaphoreType.DMA,
        ],
        compiler_params=params,
    )(routes, returned, patches, client_in, client_down, x0, *saved)

    summed = comm_call(
        functools.partial(total_kernel, n),
        shape((pack_rows, width), F32), vmem(), vmem(),
        [pltpu.VMEM((n, pack_rows, width), BF)], n, 3, packed,
    )
    own = width // n
    tail = summed[r_in:].reshape(ff // width + 1, PAD, width)[:, :own]
    grad_in = summed[:r_in].T
    grad_down = tail[:-1].transpose(0, 2, 1).reshape(ff, own)
    last = tail[-1].T
    patch = patches.shape[1]
    return (
        losses,
        last[:patch],
        last[width - LANES : width - LANES + TOK],
        grad_in,
        grad_down,
        parts_in[0],
        parts_down[0],
        grad_class,
    )


def solution(mesh):
    whole = P()
    in_specs = (
        P("client", None), whole, whole, whole, whole, whole, whole,
        P(None, "client", None), P(None, "client", None), whole,
    )
    out_specs = (
        P("client", None), P(None, "client"), P(None, "client"), P(None, "client"),
        P(None, "client"), P(None, "client", None), P(None, "client", None), P("client", None),
    )
    return jax.shard_map(
        per_device, mesh=mesh, in_specs=in_specs, out_specs=out_specs, check_vma=False
    )
```

time: 723 us -> 266 us (0.37); the launches traced: 713 us -> 266 us
  Pallas kernels: 0 us -> 249 us
  local copies, waits for them, and re-layouts: 242 us -> 9.11 us
  other arithmetic: 157 us -> 6.46 us
  blocking collectives: 109 us -> 0 us
  matrix products: 75.8 us -> 0 us
  waiting for transfers between devices: 66.4 us -> 0.01 us
  starting transfers between devices: 45.3 us -> 1.47 us
  between operations: 17.3 us -> 0.76 us
    pallas_call x0 -> x6, Pallas kernels: none -> 249 us  [the longest x3 202 us: comm_call(): pl.pallas_call(kernel, out_shape=out, in_specs=[in_spec], out_specs=out_s...]
    unnamed x2 -> x0, blocking collectives: 109 us -> none
    slice x7 -> x4, local copies, waits for them, and re-layouts: 87.6 us -> 1.53 us  [the longest x1 0.91 us: per_device(): tail = summed[r_in:].reshape(ff // width + 1, PAD, width)[:, :own]]
    dot_general x62 -> x0, matrix products: 75.8 us -> none  [the longest x9 13.7 us: encoder_block(): jnp.dot(normed, weight_in[:, 4 * model_width:], preferred_element_type=jn...]
    concatenate x2 -> x0, other arithmetic: 66.5 us -> none  [the longest x1 56.1 us: per_device(): blocks = jnp.concatenate([blocks_in, blocks_down, blocks_class], 1)]
    unnamed x12 -> x0, waiting for transfers between devices: 66.4 us -> none
    broadcast_in_dim x2 -> x0, local copies, waits for them, and re-layouts: 41.6 us -> none  [the longest x1 41.6 us: gather_group(): stacked = flat_rows[None]]
    select_n x3 -> x0, other arithmetic: 34.4 us -> none  [the longest x1 33 us: gather_group(): jnp.where(upper_half == 0, jnp.concatenate([stacked, partner], 0), jnp.co...]
  transfers between devices with their start and end apart: 14 -> 5, of which waited for: 4 -> 0; matrix products, arithmetic and copies ran while one was open for 49% -> 4% of each run, Pallas kernels for 0% -> 82%
where the time goes in v1:
time: 266 us
  Pallas kernels  249 us (94%)
  local copies, waits for them, and re-layouts  9.11 us (3%)
  other arithmetic  6.46 us (2%)
    pallas_call x3, Pallas kernels, comm_call(): pl.pallas_call(kernel, out_shape=out, in_specs=[in_spec], out_specs=out_s...  202 us
    pallas_call x1, Pallas kernels, per_device(): pl.pallas_call(functools.partial(server_kernel, n, group, layers, per_ima...  30.3 us
    pallas_call x1, Pallas kernels, per_device(): pl.pallas_call(functools.partial(client_backward_kernel, n, group), out_s...  10.2 us
    pallas_call x1, Pallas kernels, per_device(): pl.pallas_call(client_forward_kernel, out_shape=[shape((rows, width), BF)...  5.96 us
  transfers between devices with their start and end apart: 5, of which 0 were waited for; matrix products, arithmetic and copies ran while one was open for 4% of the time, Pallas kernels for 82%

profile of v1, /device:TPU:15, one launch (start us, length us, event | category | flops | bytes accessed | tf_op | source)
XLA Modules:
  0.0 266.4 jit_solution(24021626788644600)
XLA Ops:
  0.6 0.0 copy-start
  0.6 0.7 collective-permute-start
  1.4 0.1 collective-permute-start.1
  1.5 1.5 copy.18.patch_ref
  3.0 0.0 copy-done
  3.0 0.1 copy.19
  3.2 6.0 %shard_map.161 = (bf16[128,384]{1,0:T(8,128)(2,1)}, f32[128,384]{1,0:T(8,128)}, f32[128,1152]{1,0:T(8,128)}, bf16[6,128,128]{2,1,0:T(8,128)(2,1)}, bf16[128,384]...) custom-call(bf16[128,192]{1,0:T(8,128)(2,1)} %copy.18.patch_ref, bf16[192,384]{1,0:T(8,128)(2,1)} %embed_ref.1, ...), custom_call_target="tpu_custom_call" | custom-call | tf_op jit(solution)/shard_map/pallas_call | solution.py:571
  9.2 43.1 %shard_map.162.refs_2_ = bf16[32,64,384]{2,1,0:T(8,128)(2,1)} custom-call(bf16[2,64,384]{2,1,0:T(8,128)(2,1)} %bitcast.25), custom_call_target="tpu_custom_call" | custom-call | tf_op jit(solution)/shard_map/pallas_call | solution.py:505
  52.3 0.7 pad.4.refs_3_
  52.9 0.0 collective-permute-done.1.refs_7_
  52.9 0.0 collective-permute-done.refs_5_
  52.9 0.0 copy-start.1
  52.9 1.4 copy-done.1
  54.3 30.3 %shard_map.163 = (f32[1,16]{1,0:T(1,128)}, bf16[32,64,384]{2,1,0:T(8,128)(2,1)}, bf16[384,128]{1,0:T(8,128)(2,1)}, bf16[2,192,3072]{2,1,0:T(8,128)(2,1)}, bf16[2...) custom-call(s32[32]{0:T(128)} %bitcast.27, s32[256]{0:T(256)} %refs_1_.1, ...), custom_call_target="tpu_custom_call" | custom-call | tf_op jit(solution)/shard_map/pallas_call | solution.py:591
  84.6 0.1 collective-permute-start.2
  84.7 0.5 collective-permute-start.3
  85.2 0.1 collective-permute-start.4
  85.3 40.6 %shard_map.164.back_ref = bf16[32,64,384]{2,1,0:T(8,128)(2,1)} custom-call(bf16[32,64,384]{2,1,0:T(8,128)(2,1)} %get-tuple-element.24.in_ref), custom_call_target="tpu_custom_call" | custom-call | tf_op jit(solution)/shard_map/pallas_call | solution.py:505
  125.9 10.2 %shard_map.165.in_ref = bf16[32,176,384]{2,1,0:T(8,128)(2,1)} custom-call(s32[32]{0:T(128)} %bitcast.28, bf16[32,64,384]{2,1,0:T(8,128)(2,1)} %shard_map.164.back_ref, bf16[128,192]{1,0:T(8,128)(2,1)} %copy.18.patch_ref, bf16[384,3072]{1,0:T(8,128)(2,1)} %w_ref.3, bf16[1536,384]{1,0:T(8,128)(2,1)} %d_ref.3, f32[128,384]{1,0:T(8,128)} %get-tuple-element.25.x_ref, ...), custom_call_target="tpu_custom_call" | custom-call | tf_op jit(solution)/shard_map/pallas_call | solution.py:649
  136.1 0.0 copy-start.3
  136.1 118.4 %shard_map.166 = f32[176,384]{1,0:T(8,128)} custom-call(bf16[32,176,384]{2,1,0:T(8,128)(2,1)} %shard_map.165.in_ref), custom_call_target="tpu_custom_call" | custom-call | tf_op jit(solution)/shard_map/pallas_call | solution.py:505
  254.6 0.9 slice.24
  255.5 1.6 slice_bitcast_fusion
  257.1 0.1 copy.25
  257.2 0.6 slice.33
  257.9 0.6 copy.26
  258.6 0.7 copy.23
  259.2 0.0 collective-permute-done.4
  259.2 0.0 copy-done.3
  259.3 0.7 copy.24
  260.0 0.0 collective-permute-done.3
  260.0 0.0 copy-start.2
  260.0 3.4 %convert_add_fusion.1 = f32[2,768,384]{2,1,0:T(8,128)} fusion(bf16[2,768,384]{2,1,0:T(8,128)(2,1)} %collective-permute-done.3, bf16[2,768,384]{2,1,0:T(8,128)(2,1)} %get-tuple-element.33), kind=kLoop, calls=%fused_computation.1 | loop fusion | flops 1769472 | bytes 4718592 | tf_op jit(solution)/shard_map/add | solution.py:638
  263.4 0.0 collective-permute-done.2
  263.4 0.0 copy-done.2
  263.4 3.0 %convert_add_fusion = f32[2,192,3072]{2,1,0:T(8,128)} fusion(bf16[2,192,3072]{2,1,0:T(8,128)(2,1)S(1)} %collective-permute-done.2, bf16[2,192,3072]{2,1,0:T(8,128)(2,1)S(1)} %copy-done.2), kind=kLoop, calls=%fused_computation | loop fusion | flops 3538944 | bytes 9437184 | tf_op jit(solution)/shard_map/add | solution.py:634
  (7 shorter events, 0.1 us)
Async XLA Ops:
  0.6 2.4 copy-start
  0.6 52.3 %collective-permute-start = (bf16[2,192,3072]{2,1,0:T(8,128)(2,1)}, bf16[2,192,3072]{2,1,0:T(8,128)(2,1)S(1)}, u32[]{:S(2)}, u32[]{:S(2)}) collective-permute-start(bf16[2,192,3072]{2,1,0:T(8,128)(2,1)} %refs_4_.1), channel_id=1, source_target_pairs={{0,1},{1,0},{2,3},{3,2},{4,5},{5,4},{6,7},{7,6},{8,9},{9,8},{10,11... | collective-permute-start | bytes 7077896 | tf_op jit(solution)/shard_map/ppermute | solution.py:528
  1.4 51.5 %collective-permute-start.1 = (bf16[2,768,384]{2,1,0:T(8,128)(2,1)}, bf16[2,768,384]{2,1,0:T(8,128)(2,1)}, u32[]{:S(2)}, u32[]{:S(2)}) collective-permute-start(bf16[2,768,384]{2,1,0:T(8,128)(2,1)} %refs_6_.1), channel_id=1, source_target_pairs={{0,1},{1,0},{2,3},{3,2},{4,5},{5,4},{6,7},{7,6},{8,9},{9,8},{10,11... | collective-permute-start | bytes 3538952 | tf_op jit(solution)/shard_map/ppermute | solution.py:528
  52.9 1.4 copy-start.1
  84.6 178.7 %collective-permute-start.2 = (bf16[2,192,3072]{2,1,0:T(8,128)(2,1)}, bf16[2,192,3072]{2,1,0:T(8,128)(2,1)S(1)}, u32[]{:S(2)}, u32[]{:S(2)}) collective-permute-start(bf16[2,192,3072]{2,1,0:T(8,128)(2,1)} %get-tuple-element.32), channel_id=1, source_target_pairs={{0,1},{1,0},{2,3},{3,2},{4,5},{5,4},{6,7},{7,6},{8,9},{9,8},{10,11... | collective-permute-start | bytes 7077896 | tf_op jit(solution)/shard_map/ppermute | solution.py:528
  84.7 175.2 %collective-permute-start.3 = (bf16[2,768,384]{2,1,0:T(8,128)(2,1)}, bf16[2,768,384]{2,1,0:T(8,128)(2,1)}, u32[]{:S(2)}, u32[]{:S(2)}) collective-permute-start(bf16[2,768,384]{2,1,0:T(8,128)(2,1)} %get-tuple-element.34), channel_id=1, source_target_pairs={{0,1},{1,0},{2,3},{3,2},{4,5},{5,4},{6,7},{7,6},{8,9},{9,8},{10,11... | collective-permute-start | bytes 3538952 | tf_op jit(solution)/shard_map/ppermute | solution.py:528
  85.2 174.0 %collective-permute-start.4 = (bf16[384,128]{1,0:T(8,128)(2,1)}, bf16[384,128]{1,0:T(8,128)(2,1)S(1)}, u32[]{:S(2)}, u32[]{:S(2)}) collective-permute-start(bf16[384,128]{1,0:T(8,128)(2,1)} %get-tuple-element.35), channel_id=1, source_target_pairs={{0,1},{1,0},{2,3},{3,2},{4,5},{5,4},{6,7},{7,6},{8,9},{9,8},{10,11... | collective-permute-start | bytes 294920 | tf_op jit(solution)/shard_map/ppermute | solution.py:528
  136.1 123.1 %copy-start.3 = (bf16[384,128]{1,0:T(8,128)(2,1)S(1)}, bf16[384,128]{1,0:T(8,128)(2,1)}, u32[]{:S(2)}) copy-start(bf16[384,128]{1,0:T(8,128)(2,1)} %get-tuple-element.35) | copy-start | bytes 294916
  260.0 3.4 %copy-start.2 = (bf16[2,192,3072]{2,1,0:T(8,128)(2,1)S(1)}, bf16[2,192,3072]{2,1,0:T(8,128)(2,1)}, u32[]{:S(2)}) copy-start(bf16[2,192,3072]{2,1,0:T(8,128)(2,1)} %get-tuple-element.31) | copy-start | bytes 7077892
